TPU v7x, 32 devices: a whole 2x2x4 slice. The times are simulated.
32 devices in a mesh: exp: 8 (over y, x, core), tp: 4 (over z).
Axes of the slice: x: 2, y: 2, z: 4, core: 2. Of those that a mesh axis runs over, the one named last changes fastest.
Arguments:
- tokens: bfloat16 [224, 4096], P('exp', 'tp'), may hold values from -6 to 6
- cotangent: bfloat16 [224, 4096], P('exp', 'tp'), may hold values from -6 to 6
- experts: int32 [224, 2], P('exp'), may hold values from 0 to 7, all different within a row; in each aligned block of 28 rows (0 to 27, 28 to 55, ...) at most 8 rows name the same one
- gates: float32 [224, 2], P('exp'), may hold values from 0.1 to 0.9
- w_gate: bfloat16 [8, 4096, 8192], P('exp', None, 'tp'), may hold values from -0.09375 to 0.09375
- w_up: bfloat16 [8, 4096, 8192], P('exp', None, 'tp'), may hold values from -0.09375 to 0.09375
- w_down: bfloat16 [8, 8192, 4096], P('exp', 'tp'), may hold values from -0.0625 to 0.0625
Outputs:
- output: bfloat16 [224, 4096], P('exp', 'tp')
- input_grad: bfloat16 [224, 4096], P('exp', 'tp')
- grad_gate: bfloat16 [8, 4096, 8192], P('exp', None, 'tp')
- grad_up: bfloat16 [8, 4096, 8192], P('exp', None, 'tp')
- grad_down: bfloat16 [8, 8192, 4096], P('exp', 'tp')
Inputs may be any that keep to these rules, and one draw needn't show every extreme that they name: Each row names 2 different experts. In each aligned block of 28 rows (the rows of one index of exp) no expert is named by more than 8 rows, and in some blocks one is named by exactly 8.
All inputs are finite; a program needn't handle non-finite values.
Results may differ from a plain program's by a relative error of at most 0.017.
Values may be sent and summed in bfloat16 or wider, within the bound.
A program may use at most 192 MiB of HBM per device.

v0:
```python
import jax
import jax.numpy as jnp
from jax import lax
from jax.sharding import PartitionSpec as P

EXPERTS = 8
CAP = 8


def contract_rows(left, right):
    return lax.dot_general(
        left, right, (((0,), (0,)), ((), ())), preferred_element_type=jnp.float32
    )


def contract_cols(left, right):
    return lax.dot_general(
        left, right, (((1,), (1,)), ((), ())), preferred_element_type=jnp.float32
    )


def slot_places(experts, capacity):
    pair_ids = experts.reshape(-1)
    matches = (pair_ids[:, None] == jnp.arange(EXPERTS, dtype=jnp.int32)[None, :]).astype(jnp.int32)
    before = jnp.cumsum(matches, axis=0) - matches
    slot_ids = jnp.sum(before * matches, axis=1)
    return pair_ids * capacity + slot_ids


def per_device(tokens, cotangent, experts, gates, w_gate, w_up, w_down):
    exp_devices = lax.axis_size("exp")
    group_size = exp_devices // EXPERTS
    capacity = CAP
    tok_rows, top_count = experts.shape
    model_width = w_gate.shape[1]
    gate_mat = w_gate[0]
    up_mat = w_up[0]
    down_mat = w_down[0]
    row_count = exp_devices * capacity
    places = slot_places(experts, capacity)
    pick_table = (
        places[:, None] == jnp.arange(EXPERTS * capacity, dtype=jnp.int32)[None, :]
    ).astype(jnp.float32)
    per_token = pick_table.reshape(tok_rows, top_count, EXPERTS * capacity)
    weighted = jnp.sum(per_token * gates[:, :, None], axis=1)
    unweighted = jnp.sum(per_token, axis=1)
    pick_low = pick_table.astype(jnp.bfloat16)
    scaled = (gates[:, :, None] * cotangent[:, None, :].astype(jnp.float32)).astype(jnp.bfloat16)
    scaled = scaled.reshape(tok_rows * top_count, cotangent.shape[1])

    def merge_group(received):
        col_count = received.shape[2]
        summed = jnp.sum(received.reshape(EXPERTS, group_size, capacity, col_count), axis=1)
        return summed.reshape(EXPERTS * capacity, col_count)

    def gather_tokens(table, received):
        return jnp.dot(
            table,
            merge_group(received),
            precision=lax.Precision.HIGHEST,
            preferred_element_type=jnp.float32,
        )

    whole_tokens, whole_scaled = (
        lax.all_gather(tokens, "tp", axis=1, tiled=True),
        lax.all_gather(scaled, "tp", axis=1, tiled=True),
    )
    col_count = whole_tokens.shape[1]
    repeated = jnp.repeat(whole_tokens, top_count, axis=0)
    token_send = contract_rows(pick_low, repeated).astype(jnp.bfloat16)
    grad_send = contract_rows(pick_low, whole_scaled).astype(jnp.bfloat16)
    token_send = jnp.broadcast_to(
        token_send.reshape(EXPERTS, 1, capacity, col_count),
        (EXPERTS, group_size, capacity, col_count),
    )
    grad_send = jnp.broadcast_to(
        grad_send.reshape(EXPERTS, 1, capacity, col_count),
        (EXPERTS, group_size, capacity, col_count),
    )
    token_send, grad_send = (
        token_send.reshape(exp_devices, capacity, col_count),
        grad_send.reshape(exp_devices, capacity, col_count),
    )
    token_rows, cot_rows = (
        lax.all_to_all(token_send, "exp", split_axis=0, concat_axis=0, tiled=True),
        lax.all_to_all(grad_send, "exp", split_axis=0, concat_axis=0, tiled=True),
    )
    token_rows = token_rows.reshape(row_count, model_width)
    cot_rows = cot_rows.reshape(row_count, model_width)
    hidden_gate = jnp.dot(token_rows, gate_mat, preferred_element_type=jnp.float32)
    hidden_up = jnp.dot(token_rows, up_mat, preferred_element_type=jnp.float32)
    grad_act = contract_cols(cot_rows, down_mat)
    sigmoid_gate = jax.nn.sigmoid(hidden_gate)
    activation = (hidden_gate * sigmoid_gate * hidden_up).astype(jnp.bfloat16)
    out_term = jnp.dot(activation, down_mat, preferred_element_type=jnp.float32)
    grad_first = (
        grad_act * hidden_up * sigmoid_gate * (1.0 + hidden_gate * (1.0 - sigmoid_gate))
    ).astype(jnp.bfloat16)
    grad_second = (grad_act * hidden_gate * sigmoid_gate).astype(jnp.bfloat16)
    grad_down = contract_rows(activation, cot_rows).astype(jnp.bfloat16)
    grad_gate = contract_rows(token_rows, grad_first).astype(jnp.bfloat16)
    grad_up = contract_rows(token_rows, grad_second).astype(jnp.bfloat16)
    back_term = contract_cols(grad_first, gate_mat) + contract_cols(grad_second, up_mat)
    out_back, grad_back = (
        lax.all_to_all(
            out_term.reshape(exp_devices, capacity, model_width),
            "exp",
            split_axis=0,
            concat_axis=0,
            tiled=True,
        ),
        lax.all_to_all(
            back_term.reshape(exp_devices, capacity, model_width),
            "exp",
            split_axis=0,
            concat_axis=0,
            tiled=True,
        ),
    )
    out_tokens = gather_tokens(weighted, out_back)
    grad_tokens = gather_tokens(unweighted, grad_back)
    output, input_grad = (
        lax.psum_scatter(
            out_tokens.astype(jnp.bfloat16), "tp", scatter_dimension=1, tiled=True
        ).astype(jnp.float32),
        lax.psum_scatter(
            grad_tokens.astype(jnp.bfloat16), "tp", scatter_dimension=1, tiled=True
        ).astype(jnp.float32),
    )
    return (
        output.astype(jnp.bfloat16),
        input_grad.astype(jnp.bfloat16),
        grad_gate[None],
        grad_up[None],
        grad_down[None],
    )


def solution(mesh):
    in_specs = (
        P("exp", "tp"),
        P("exp", "tp"),
        P("exp", None),
        P("exp", None),
        P("exp", None, "tp"),
        P("exp", None, "tp"),
        P("exp", "tp", None),
    )
    out_specs = (
        P("exp", "tp"),
        P("exp", "tp"),
        P("exp", None, "tp"),
        P("exp", None, "tp"),
        P("exp", "tp", None),
    )
    return jax.shard_map(
        per_device, mesh=mesh, in_specs=in_specs, out_specs=out_specs, check_vma=False
    )
```

profile of v0, /device:TPU:0, one launch (start us, length us, event | category | flops | bytes accessed | tf_op | source)
XLA Modules:
  0.0 172.2 jit_solution(9109463998063205250)
XLA Ops:
  7.2 0.8 copy.30
  7.9 0.1 mul.77
  8.0 0.8 copy.27
  9.1 0.2 select_reduce_fusion.1
  9.3 0.9 mul.79
  10.2 0.2 mul.80
  10.4 16.8 %all_gather.7 = bf16[56,4096]{1,0:T(8,128)(2,1)S(1)} all-gather(bf16[56,1024]{1,0:T(8,128)(2,1)S(1)} %multiply_convert_fusion.3), channel_id=1, replica_groups=mesh['exp'=8,'tp'=4] {'tp'}, dimensions={1}, use_global_device_ids=true | all-gather | bytes 573440 | tf_op jit(solution)/shard_map/all_gather | solution.py:66
  27.2 1.2 fusion.19
  28.4 3.7 %all-to-all-start.2 = ((bf16[8,8,4096]{2,1,0:T(8,128)(2,1)}), bf16[8,8,4096]{2,1,0:T(8,128)(2,1)S(1)}, u32[]{:S(2)}, u32[]{:S(2)}) async-start(bf16[8,8,4096]{2,1,0:T(8,128)(2,1)} %fusion.19), calls=%async_computation.3 | async-start | bytes 1048576 | tf_op jit(solution)/shard_map/all_to_all | solution.py:86
  32.3 14.9 %all_gather.6 = bf16[28,4096]{1,0:T(8,128)(2,1)S(1)} all-gather(bf16[28,1024]{1,0:T(8,128)(2,1)} %param.7), channel_id=1, replica_groups=mesh['exp'=8,'tp'=4] {'tp'}, dimensions={1}, use_global_device_ids=true | all-gather | bytes 286720 | tf_op jit(solution)/shard_map/all_gather | solution.py:65
  47.2 0.4 broadcast_in_dim.8
  47.6 0.2 reshape.64
  47.8 1.2 fusion.18
  49.0 3.9 %all-to-all-start = ((bf16[8,8,4096]{2,1,0:T(8,128)(2,1)}), bf16[8,8,4096]{2,1,0:T(8,128)(2,1)S(1)}, u32[]{:S(2)}, u32[]{:S(2)}) async-start(bf16[8,8,4096]{2,1,0:T(8,128)(2,1)} %fusion.18), calls=%async_computation | async-start | bytes 1048576 | tf_op jit(solution)/shard_map/all_to_all | solution.py:85
  52.9 11.0 %fusion.2 = f32[64,2048]{1,0:T(8,128)S(1)} fusion(bf16[1,2048,4096]{2,1,0:T(8,128)(2,1)} %param.13, bf16[8,8,4096]{2,1,0:T(8,128)(2,1)S(1)} %all-to-all-done.2), kind=kOutput, calls=%fused_computation.2 | convolution fusion | flops 1073741824 | bytes 17825792 | tf_op jit(solution)/shard_map/dot_general | solution.py:17
  63.9 8.9 %fusion.6 = f32[64,2048]{1,0:T(8,128)S(1)} fusion(bf16[1,4096,2048]{2,1,0:T(8,128)(2,1)} %param.12, bf16[8,8,4096]{2,1,0:T(8,128)(2,1)S(1)} %all-to-all-done), kind=kOutput, calls=%fused_computation.6 | convolution fusion | flops 1073741824 | bytes 17825792 | tf_op jit(solution)/shard_map/dot_general | solution.py:91
  72.9 10.0 %multiply_convert_fusion.1 = (bf16[64,2048]{1,0:T(8,128)(2,1)}, bf16[64,2048]{1,0:T(8,128)(2,1)S(1)}, bf16[64,2048]{1,0:T(8,128)(2,1)}) fusion(f32[64,2048]{1,0:T(8,128)S(1)} %fusion.2, f32[64,2048]{1,0:T(8,128)S(1)} %fusion.6, bf16[1,4096,2048]{2,1,0:T(8,128)(2,1)} %param.11, bf16[8,8,4096]{2,1,0:T(8,128)(2,1)S(1)} %all-to-all-done), kind=kOutput, calls=%fused_computation.32 | convolution fusion | flops 1075838976 | bytes 19136512 | tf_op jit(solution)/shard_map/dot_general | solution.py:90
  82.9 4.0 %fusion = f32[8,8,4096]{2,1,0:T(8,128)} fusion(bf16[1,2048,4096]{2,1,0:T(8,128)(2,1)S(1)} %bitcast.69, bf16[64,2048]{1,0:T(8,128)(2,1)S(1)} %get-tuple-element.8), kind=kOutput, calls=%fused_computation | convolution fusion | flops 1073741824 | bytes 18087936 | tf_op jit(solution)/shard_map/dot_general | solution.py:95
  86.9 4.2 %all-to-all-start.1 = ((f32[8,8,4096]{2,1,0:T(8,128)}), f32[8,8,4096]{2,1,0:T(8,128)S(1)}, u32[]{:S(2)}, u32[]{:S(2)}) async-start(f32[8,8,4096]{2,1,0:T(8,128)} %fusion), calls=%async_computation.1 | async-start | bytes 2097152 | tf_op jit(solution)/shard_map/all_to_all | solution.py:105
  91.1 11.0 %fusion.4 = f32[64,4096]{1,0:T(8,128)S(1)} fusion(bf16[64,2048]{1,0:T(8,128)(2,1)} %get-tuple-element.9, bf16[1,4096,2048]{2,1,0:T(8,128)(2,1)} %param.12), kind=kOutput, calls=%fused_computation.4 | convolution fusion | flops 1073741824 | bytes 18087936 | tf_op jit(solution)/shard_map/dot_general | solution.py:17
  102.2 12.0 %fusion.15 = f32[8,8,4096]{2,1,0:T(8,128)} fusion(f32[64,4096]{1,0:T(8,128)S(1)} %fusion.4, bf16[64,2048]{1,0:T(8,128)(2,1)} %get-tuple-element.7, bf16[1,4096,2048]{2,1,0:T(8,128)(2,1)} %param.11), kind=kOutput, calls=%fused_computation.16 | convolution fusion | flops 1074003968 | bytes 19136512 | tf_op jit(solution)/shard_map/dot_general | solution.py:17
  114.2 4.2 %all-to-all-start.3 = ((f32[8,8,4096]{2,1,0:T(8,128)}), f32[8,8,4096]{2,1,0:T(8,128)S(1)}, u32[]{:S(2)}, u32[]{:S(2)}) async-start(f32[8,8,4096]{2,1,0:T(8,128)} %fusion.15), calls=%async_computation.4 | async-start | bytes 2097152 | tf_op jit(solution)/shard_map/all_to_all | solution.py:112
  118.5 0.1 copy.29
  118.6 0.1 convert_reduce_fusion
  118.7 1.3 convolution_convert_fusion.3
  120.1 0.3 reduce-scatter.5.cloned.1.call-start
  120.4 9.5 %convert_bitcast_fusion.2 = bf16[1,4096,2048]{2,1,0:T(8,128)(2,1)} fusion(bf16[64,2048]{1,0:T(8,128)(2,1)} %get-tuple-element.7, bf16[8,8,4096]{2,1,0:T(8,128)(2,1)S(1)} %all-to-all-done), kind=kOutput, calls=%fused_computation.14 | convolution fusion | flops 1082130432 | bytes 17563648 | tf_op jit(solution)/shard_map/dot_general | solution.py:11
  129.9 3.9 %all-to-all-done.3 = f32[8,8,4096]{2,1,0:T(8,128)S(1)} async-done(((f32[8,8,4096]{2,1,0:T(8,128)}), f32[8,8,4096]{2,1,0:T(8,128)S(1)}, u32[]{:S(2)}, u32[]{:S(2)}) %all-to-all-start.3) | async-done | bytes 1048608 | tf_op jit(solution)/shard_map/all_to_all | solution.py:112
  133.8 1.3 convolution_convert_fusion.2
  135.1 8.5 %convert_bitcast_fusion.1 = bf16[1,4096,2048]{2,1,0:T(8,128)(2,1)} fusion(bf16[64,2048]{1,0:T(8,128)(2,1)S(1)} %copy-done, bf16[8,8,4096]{2,1,0:T(8,128)(2,1)S(1)} %all-to-all-done), kind=kOutput, calls=%fused_computation.13 | convolution fusion | flops 1082130432 | bytes 17563648 | tf_op jit(solution)/shard_map/dot_general | solution.py:11
  143.7 8.5 %convert_bitcast_fusion = bf16[1,2048,4096]{2,1,0:T(8,128)(2,1)} fusion(bf16[64,2048]{1,0:T(8,128)(2,1)S(1)} %get-tuple-element.8, bf16[8,8,4096]{2,1,0:T(8,128)(2,1)S(1)} %all-to-all-done.2), kind=kOutput, calls=%fused_computation.12 | convolution fusion | flops 1082130432 | bytes 17563648 | tf_op jit(solution)/shard_map/dot_general | solution.py:11
  152.2 13.1 %reduce-scatter.5.cloned.1.call-done = bf16[28,1024]{1,0:T(8,128)(2,1)} async-done(((bf16[28,4096]{1,0:T(8,128)(2,1)}), bf16[28,1024]{1,0:T(8,128)(2,1)}) %reduce-scatter.5.cloned.1.call-update) | async-done | bytes 57360 | tf_op jit(solution)/shard_map/reduce_scatter | solution.py:126
  (28 shorter events, 0.6 us)
Async XLA Ops:
  28.4 20.6 %all-to-all-start.2 = ((bf16[8,8,4096]{2,1,0:T(8,128)(2,1)}), bf16[8,8,4096]{2,1,0:T(8,128)(2,1)S(1)}, u32[]{:S(2)}, u32[]{:S(2)}) async-start(bf16[8,8,4096]{2,1,0:T(8,128)(2,1)} %fusion.19), calls=%async_computation.3 | async-start | bytes 1048576 | tf_op jit(solution)/shard_map/all_to_all | solution.py:86
  49.0 14.9 %all-to-all-start = ((bf16[8,8,4096]{2,1,0:T(8,128)(2,1)}), bf16[8,8,4096]{2,1,0:T(8,128)(2,1)S(1)}, u32[]{:S(2)}, u32[]{:S(2)}) async-start(bf16[8,8,4096]{2,1,0:T(8,128)(2,1)} %fusion.18), calls=%async_computation | async-start | bytes 1048576 | tf_op jit(solution)/shard_map/all_to_all | solution.py:85
  63.9 18.9 %slice-start = ((s8[16777216]{0:T(1024)(128)(4,1)}), s8[4194304]{0:T(1024)(128)(4,1)S(1)}, s32[]{:S(2)}) async-start(s8[16777216]{0:T(1024)(128)(4,1)} %bitcast.68), calls=%async_computation.8 | async-start | bytes 8388608
  63.9 18.9 %slice-start.1 = ((s8[16777216]{0:T(1024)(128)(4,1)}), s8[4194304]{0:T(1024)(128)(4,1)S(1)}, s32[]{:S(2)}) async-start(s8[16777216]{0:T(1024)(128)(4,1)} %bitcast.68), calls=%async_computation.9 | async-start | bytes 8388608
  72.9 10.0 %slice-start.2 = ((s8[16777216]{0:T(1024)(128)(4,1)}), s8[4194304]{0:T(1024)(128)(4,1)S(1)}, s32[]{:S(2)}) async-start(s8[16777216]{0:T(1024)(128)(4,1)} %bitcast.68), calls=%async_computation.10 | async-start | bytes 8388608
  72.9 10.0 %slice-start.3 = ((s8[16777216]{0:T(1024)(128)(4,1)}), s8[4194304]{0:T(1024)(128)(4,1)S(1)}, s32[]{:S(2)}) async-start(s8[16777216]{0:T(1024)(128)(4,1)} %bitcast.68), calls=%async_computation.11 | async-start | bytes 8388608
  86.9 27.3 %all-to-all-start.1 = ((f32[8,8,4096]{2,1,0:T(8,128)}), f32[8,8,4096]{2,1,0:T(8,128)S(1)}, u32[]{:S(2)}, u32[]{:S(2)}) async-start(f32[8,8,4096]{2,1,0:T(8,128)} %fusion), calls=%async_computation.1 | async-start | bytes 2097152 | tf_op jit(solution)/shard_map/all_to_all | solution.py:105
  91.1 27.3 %copy-start.1 = (s32[28,2]{0,1:T(2,128)S(1)}, s32[28,2]{0,1:T(2,128)}, u32[]{:S(2)}) copy-start(s32[28,2]{0,1:T(2,128)} %param.9) | copy-start | bytes 676
  114.2 19.6 %all-to-all-start.3 = ((f32[8,8,4096]{2,1,0:T(8,128)}), f32[8,8,4096]{2,1,0:T(8,128)S(1)}, u32[]{:S(2)}, u32[]{:S(2)}) async-start(f32[8,8,4096]{2,1,0:T(8,128)} %fusion.15), calls=%async_computation.4 | async-start | bytes 2097152 | tf_op jit(solution)/shard_map/all_to_all | solution.py:112
  118.4 33.8 %reduce-scatter.3.cloned.1.call-start = ((), (), s32[]{:S(2)}) async-start(), calls=%async_computation.6 | async-start | bytes 327680 | tf_op jit(solution)/shard_map/reduce_scatter | solution.py:123
  120.1 15.1 %copy-start = (bf16[64,2048]{1,0:T(8,128)(2,1)S(1)}, bf16[64,2048]{1,0:T(8,128)(2,1)}, u32[]{:S(2)}) copy-start(bf16[64,2048]{1,0:T(8,128)(2,1)} %get-tuple-element.9) | copy-start | bytes 786436
  120.1 45.3 %reduce-scatter.5.cloned.1.call-start = ((), (), s32[]{:S(2)}) async-start(), calls=%async_computation.7 | async-start | bytes 327680 | tf_op jit(solution)/shard_map/reduce_scatter | solution.py:126
Sparse Core Ops, SparseCore 0:
  122.0 22.2 reduce-scatter.2
  147.1 18.1 reduce-scatter.4
where the time goes:
time: 173 us; the launch traced here: 172 us
  matrix products  88.6 us (51%)
  blocking collectives  31.7 us (18%)
  waiting for transfers between devices  17 us (10%)
  starting transfers between devices  16.4 us (9%)
  between operations  14.2 us (8%)
  local copies, waits for them, and re-layouts  3.7 us (2%)
    dot_general x3, matrix products, contract_cols(): lax.dot_general(left, right, (((1,), (1,)), ((), ())), preferred_element_...  34 us
    dot_general x5, matrix products, contract_rows(): lax.dot_general(left, right, (((0,), (0,)), ((), ())), preferred_element_...  29 us
    all_gather x1, blocking collectives, per_device(): lax.all_gather(scaled, 'tp', axis=1, tiled=True)  16.8 us
    all_gather x1, blocking collectives, per_device(): lax.all_gather(tokens, 'tp', axis=1, tiled=True)  14.9 us
    reduce_scatter x1, waiting for transfers between devices, per_device(): lax.psum_scatter(grad_tokens.astype(jnp.bfloat16), 'tp', scatter_dimensio...  13.1 us
    dot_general x1, matrix products, per_device(): jnp.dot(token_rows, gate_mat, preferred_element_type=jnp.float32)  9.95 us
    dot_general x1, matrix products, per_device(): hidden_up = jnp.dot(token_rows, up_mat, preferred_element_type=jnp.float32)  8.94 us
    all_to_all x1, starting transfers between devices, per_device(): lax.all_to_all(out_term.reshape(exp_devices, capacity, model_width), 'exp...  4.21 us
  transfers between devices with their start and end apart: 6, of which 2 were waited for; matrix products, arithmetic and copies ran while one was open for 38% of the time, Pallas kernels for 0%

commit v1 on v0

--- a/solution.py
+++ b/solution.py
@@ -5,6 +5,27 @@
 
 EXPERTS = 8
 CAP = 8
+
+
+def in_order(tiles, dim):
+    tiles = jnp.moveaxis(tiles, 0, dim)
+    lengths = tiles.shape
+    return tiles.reshape(*lengths[:dim], lengths[dim] * lengths[dim + 1], *lengths[dim + 2 :])
+
+
+def collected_by_bits(x, axis):
+    size, index = (lax.axis_size(axis), lax.axis_index(axis))
+    parts, distance = (x[None], 1)
+    while distance < size:
+        theirs = lax.ppermute(parts, axis, [(i, i ^ distance) for i in range(size)])
+        low = index & distance == 0
+        parts = jnp.concatenate([jnp.where(low, parts, theirs), jnp.where(low, theirs, parts)])
+        distance *= 2
+    return parts
+
+
+def collect(x, axis, dim):
+    return in_order(collected_by_bits(x, axis), dim)
 
 
 def contract_rows(left, right):
@@ -62,7 +83,7 @@
         )
 
     whole_tokens, whole_scaled = (
-        lax.all_gather(tokens, "tp", axis=1, tiled=True),
+        collect(tokens, "tp", 1),
         lax.all_gather(scaled, "tp", axis=1, tiled=True),
     )
     col_count = whole_tokens.shape[1]

time: 173 us -> 166 us (0.960)
  blocking collectives: 31.7 us -> 14.9 us
  waiting for transfers between devices: 17 us -> 22.8 us
  starting transfers between devices: 16.4 us -> 19.8 us
    all_gather x1 -> x0, blocking collectives: 14.9 us -> none  [per_device(): lax.all_gather(tokens, 'tp', axis=1, tiled=True)]
    all_to_all x1, waiting for transfers between devices: 0.01 us -> 5.82 us  [per_device(): lax.all_to_all(grad_send, 'exp', split_axis=0, concat_axis=0, tiled=True)]
    ppermute x0 -> x2, starting transfers between devices: none -> 3.9 us  [collected_by_bits(): theirs = lax.ppermute(parts, axis, [(i, i ^ distance) for i in range(size)])]
    all_gather x1, blocking collectives: 16.8 us -> 14.9 us  [per_device(): lax.all_gather(scaled, 'tp', axis=1, tiled=True)]
  transfers between devices with their start and end apart: 6 -> 8, of which waited for: 2 -> 4; matrix products, arithmetic and copies ran while one was open for 38% -> 42% of each run, Pallas kernels for 0% -> 0%
where the time goes in v1:
time: 166 us
  matrix products  88.6 us (53%)
  waiting for transfers between devices  22.8 us (14%)
  starting transfers between devices  19.8 us (12%)
  blocking collectives  14.9 us (9%)
  between operations  14.3 us (9%)
  local copies, waits for them, and re-layouts  4.06 us (2%)
    dot_general x3, matrix products, contract_cols(): lax.dot_general(left, right, (((1,), (1,)), ((), ())), preferred_element_...  34 us
    dot_general x5, matrix products, contract_rows(): lax.dot_general(left, right, (((0,), (0,)), ((), ())), preferred_element_...  29 us
    all_gather x1, blocking collectives, per_device(): lax.all_gather(scaled, 'tp', axis=1, tiled=True)  14.9 us
    reduce_scatter x1, waiting for transfers between devices, per_device(): lax.psum_scatter(grad_tokens.astype(jnp.bfloat16), 'tp', scatter_dimensio...  11.6 us
    dot_general x1, matrix products, per_device(): jnp.dot(token_rows, gate_mat, preferred_element_type=jnp.float32)  9.93 us
    dot_general x1, matrix products, per_device(): hidden_up = jnp.dot(token_rows, up_mat, preferred_element_type=jnp.float32)  8.94 us
    all_to_all x1, waiting for transfers between devices, per_device(): lax.all_to_all(grad_send, 'exp', split_axis=0, concat_axis=0, tiled=True)  5.82 us
    all_to_all x1, starting transfers between devices, per_device(): lax.all_to_all(back_term.reshape(exp_devices, capacity, model_width), 'ex...  4.2 us
  transfers between devices with their start and end apart: 8, of which 4 were waited for; matrix products, arithmetic and copies ran while one was open for 42% of the time, Pallas kernels for 0%

profile of v1, /device:TPU:0, one launch (start us, length us, event | category | flops | bytes accessed | tf_op | source)
XLA Modules:
  0.0 165.9 jit_solution(5571709557808271126)
XLA Ops:
  7.2 3.1 %collective-permute-start = (bf16[1,28,1024]{2,1,0:T(8,128)(2,1)}, bf16[1,28,1024]{2,1,0:T(8,128)(2,1)S(1)}, u32[]{:S(2)}, u32[]{:S(2)}) collective-permute-start(bf16[1,28,1024]{2,1,0:T(8,128)(2,1)} %bitcast.80), channel_id=1, source_target_pairs={{0,1},{1,0},{2,3},{3,2},{4,5},{5,4},{6,7},{7,6},{8,9},{9,8},{10,11... | collective-permute-start | bytes 172040 | tf_op jit(solution)/shard_map/ppermute | solution.py:20
  10.3 0.8 copy.32
  11.2 0.8 copy.29
  12.2 0.2 select_reduce_fusion.1
  12.4 0.9 mul.79
  13.6 14.9 %all_gather.3 = bf16[56,4096]{1,0:T(8,128)(2,1)S(1)} all-gather(bf16[56,1024]{1,0:T(8,128)(2,1)S(1)} %multiply_convert_fusion.3), channel_id=1, replica_groups=mesh['exp'=8,'tp'=4] {'tp'}, dimensions={1}, use_global_device_ids=true | all-gather | bytes 573440 | tf_op jit(solution)/shard_map/all_gather | solution.py:87
  28.4 0.9 broadcast_select_fusion.3
  29.3 0.8 collective-permute-start.1
  30.1 1.2 fusion.19
  31.3 3.7 %all-to-all-start.2 = ((bf16[8,8,4096]{2,1,0:T(8,128)(2,1)}), bf16[8,8,4096]{2,1,0:T(8,128)(2,1)S(1)}, u32[]{:S(2)}, u32[]{:S(2)}) async-start(bf16[8,8,4096]{2,1,0:T(8,128)(2,1)} %fusion.19), calls=%async_computation.3 | async-start | bytes 1048576 | tf_op jit(solution)/shard_map/all_to_all | solution.py:107
  35.2 1.5 collective-permute-done.1
  36.7 0.2 copy.33
  37.1 0.4 broadcast_in_dim.22
  37.7 1.2 fusion.18
  38.9 5.8 %all-to-all-done.2 = bf16[8,8,4096]{2,1,0:T(8,128)(2,1)S(1)} async-done(((bf16[8,8,4096]{2,1,0:T(8,128)(2,1)}), bf16[8,8,4096]{2,1,0:T(8,128)(2,1)S(1)}, u32[]{:S(2)}, u32[]{:S(2)}) %all-to-all-start.2) | async-done | bytes 524320 | tf_op jit(solution)/shard_map/all_to_all | solution.py:107
  44.7 3.7 %all-to-all-start = ((bf16[8,8,4096]{2,1,0:T(8,128)(2,1)}), bf16[8,8,4096]{2,1,0:T(8,128)(2,1)S(1)}, u32[]{:S(2)}, u32[]{:S(2)}) async-start(bf16[8,8,4096]{2,1,0:T(8,128)(2,1)} %fusion.18), calls=%async_computation | async-start | bytes 1048576 | tf_op jit(solution)/shard_map/all_to_all | solution.py:106
  48.4 10.9 %fusion.2 = f32[64,2048]{1,0:T(8,128)S(1)} fusion(bf16[1,2048,4096]{2,1,0:T(8,128)(2,1)} %param.13, bf16[8,8,4096]{2,1,0:T(8,128)(2,1)S(1)} %all-to-all-done.2), kind=kOutput, calls=%fused_computation.2 | convolution fusion | flops 1073741824 | bytes 17825792 | tf_op jit(solution)/shard_map/dot_general | solution.py:38
  59.4 8.9 %fusion.6 = f32[64,2048]{1,0:T(8,128)S(1)} fusion(bf16[1,4096,2048]{2,1,0:T(8,128)(2,1)} %param.12, bf16[8,8,4096]{2,1,0:T(8,128)(2,1)S(1)} %all-to-all-done), kind=kOutput, calls=%fused_computation.6 | convolution fusion | flops 1073741824 | bytes 17825792 | tf_op jit(solution)/shard_map/dot_general | solution.py:112
  68.4 9.9 %multiply_convert_fusion.1 = (bf16[64,2048]{1,0:T(8,128)(2,1)}, bf16[64,2048]{1,0:T(8,128)(2,1)S(1)}, bf16[64,2048]{1,0:T(8,128)(2,1)}) fusion(f32[64,2048]{1,0:T(8,128)S(1)} %fusion.2, f32[64,2048]{1,0:T(8,128)S(1)} %fusion.6, bf16[1,4096,2048]{2,1,0:T(8,128)(2,1)} %param.11, bf16[8,8,4096]{2,1,0:T(8,128)(2,1)S(1)} %all-to-all-done), kind=kOutput, calls=%fused_computation.32 | convolution fusion | flops 1075838976 | bytes 19136512 | tf_op jit(solution)/shard_map/dot_general | solution.py:111
  78.3 4.0 %fusion = f32[8,8,4096]{2,1,0:T(8,128)} fusion(bf16[1,2048,4096]{2,1,0:T(8,128)(2,1)S(1)} %bitcast.77, bf16[64,2048]{1,0:T(8,128)(2,1)S(1)} %get-tuple-element.8), kind=kOutput, calls=%fused_computation | convolution fusion | flops 1073741824 | bytes 18087936 | tf_op jit(solution)/shard_map/dot_general | solution.py:116
  82.4 3.9 %all-to-all-start.1 = ((f32[8,8,4096]{2,1,0:T(8,128)}), f32[8,8,4096]{2,1,0:T(8,128)S(1)}, u32[]{:S(2)}, u32[]{:S(2)}) async-start(f32[8,8,4096]{2,1,0:T(8,128)} %fusion), calls=%async_computation.1 | async-start | bytes 2097152 | tf_op jit(solution)/shard_map/all_to_all | solution.py:126
  86.3 11.0 %fusion.4 = f32[64,4096]{1,0:T(8,128)S(1)} fusion(bf16[64,2048]{1,0:T(8,128)(2,1)} %get-tuple-element.9, bf16[1,4096,2048]{2,1,0:T(8,128)(2,1)} %param.12), kind=kOutput, calls=%fused_computation.4 | convolution fusion | flops 1073741824 | bytes 18087936 | tf_op jit(solution)/shard_map/dot_general | solution.py:38
  97.4 12.0 %fusion.15 = f32[8,8,4096]{2,1,0:T(8,128)} fusion(f32[64,4096]{1,0:T(8,128)S(1)} %fusion.4, bf16[64,2048]{1,0:T(8,128)(2,1)} %get-tuple-element.7, bf16[1,4096,2048]{2,1,0:T(8,128)(2,1)} %param.11), kind=kOutput, calls=%fused_computation.16 | convolution fusion | flops 1074003968 | bytes 19136512 | tf_op jit(solution)/shard_map/dot_general | solution.py:38
  109.4 4.2 %all-to-all-start.3 = ((f32[8,8,4096]{2,1,0:T(8,128)}), f32[8,8,4096]{2,1,0:T(8,128)S(1)}, u32[]{:S(2)}, u32[]{:S(2)}) async-start(f32[8,8,4096]{2,1,0:T(8,128)} %fusion.15), calls=%async_computation.4 | async-start | bytes 2097152 | tf_op jit(solution)/shard_map/all_to_all | solution.py:133
  113.9 1.3 convolution_convert_fusion.3
  115.3 0.3 reduce-scatter.5.cloned.1.call-start
  115.6 9.5 %convert_bitcast_fusion.2 = bf16[1,4096,2048]{2,1,0:T(8,128)(2,1)} fusion(bf16[64,2048]{1,0:T(8,128)(2,1)} %get-tuple-element.7, bf16[8,8,4096]{2,1,0:T(8,128)(2,1)S(1)} %all-to-all-done), kind=kOutput, calls=%fused_computation.14 | convolution fusion | flops 1082130432 | bytes 17563648 | tf_op jit(solution)/shard_map/dot_general | solution.py:32
  125.1 3.9 %all-to-all-done.3 = f32[8,8,4096]{2,1,0:T(8,128)S(1)} async-done(((f32[8,8,4096]{2,1,0:T(8,128)}), f32[8,8,4096]{2,1,0:T(8,128)S(1)}, u32[]{:S(2)}, u32[]{:S(2)}) %all-to-all-start.3) | async-done | bytes 1048608 | tf_op jit(solution)/shard_map/all_to_all | solution.py:133
  129.0 1.3 convolution_convert_fusion.2
  130.3 8.5 %convert_bitcast_fusion.1 = bf16[1,4096,2048]{2,1,0:T(8,128)(2,1)} fusion(bf16[64,2048]{1,0:T(8,128)(2,1)S(1)} %copy-done, bf16[8,8,4096]{2,1,0:T(8,128)(2,1)S(1)} %all-to-all-done), kind=kOutput, calls=%fused_computation.13 | convolution fusion | flops 1082130432 | bytes 17563648 | tf_op jit(solution)/shard_map/dot_general | solution.py:32
  138.9 8.5 %convert_bitcast_fusion = bf16[1,2048,4096]{2,1,0:T(8,128)(2,1)} fusion(bf16[64,2048]{1,0:T(8,128)(2,1)S(1)} %get-tuple-element.8, bf16[8,8,4096]{2,1,0:T(8,128)(2,1)S(1)} %all-to-all-done.2), kind=kOutput, calls=%fused_computation.12 | convolution fusion | flops 1082130432 | bytes 17563648 | tf_op jit(solution)/shard_map/dot_general | solution.py:32
  147.4 11.6 %reduce-scatter.5.cloned.1.call-done = bf16[28,1024]{1,0:T(8,128)(2,1)} async-done(((bf16[28,4096]{1,0:T(8,128)(2,1)}), bf16[28,1024]{1,0:T(8,128)(2,1)}) %reduce-scatter.5.cloned.1.call-update) | async-done | bytes 57360 | tf_op jit(solution)/shard_map/reduce_scatter | solution.py:147
  (38 shorter events, 1.6 us)
Async XLA Ops:
  7.2 21.3 %collective-permute-start = (bf16[1,28,1024]{2,1,0:T(8,128)(2,1)}, bf16[1,28,1024]{2,1,0:T(8,128)(2,1)S(1)}, u32[]{:S(2)}, u32[]{:S(2)}) collective-permute-start(bf16[1,28,1024]{2,1,0:T(8,128)(2,1)} %bitcast.80), channel_id=1, source_target_pairs={{0,1},{1,0},{2,3},{3,2},{4,5},{5,4},{6,7},{7,6},{8,9},{9,8},{10,11... | collective-permute-start | bytes 172040 | tf_op jit(solution)/shard_map/ppermute | solution.py:20
  29.3 7.3 %collective-permute-start.1 = (bf16[2,28,1024]{2,1,0:T(8,128)(2,1)S(1)}, bf16[2,28,1024]{2,1,0:T(8,128)(2,1)S(1)}, u32[]{:S(2)}, u32[]{:S(2)}) collective-permute-start(bf16[2,28,1024]{2,1,0:T(8,128)(2,1)S(1)} %pad_maximum_fusion), channel_id=1, source_target_pairs={{0,2},{1,3},{2,0},{3,1},{4,6},{5,7},{6,4},{7,5},{8,10},{9,11},{10,... | collective-permute-start | bytes 344072 | tf_op jit(solution)/shard_map/ppermute | solution.py:20
  31.3 13.4 %all-to-all-start.2 = ((bf16[8,8,4096]{2,1,0:T(8,128)(2,1)}), bf16[8,8,4096]{2,1,0:T(8,128)(2,1)S(1)}, u32[]{:S(2)}, u32[]{:S(2)}) async-start(bf16[8,8,4096]{2,1,0:T(8,128)(2,1)} %fusion.19), calls=%async_computation.3 | async-start | bytes 1048576 | tf_op jit(solution)/shard_map/all_to_all | solution.py:107
  44.7 14.6 %all-to-all-start = ((bf16[8,8,4096]{2,1,0:T(8,128)(2,1)}), bf16[8,8,4096]{2,1,0:T(8,128)(2,1)S(1)}, u32[]{:S(2)}, u32[]{:S(2)}) async-start(bf16[8,8,4096]{2,1,0:T(8,128)(2,1)} %fusion.18), calls=%async_computation | async-start | bytes 1048576 | tf_op jit(solution)/shard_map/all_to_all | solution.py:106
  59.4 18.9 %slice-start = ((s8[16777216]{0:T(1024)(128)(4,1)}), s8[4194304]{0:T(1024)(128)(4,1)S(1)}, s32[]{:S(2)}) async-start(s8[16777216]{0:T(1024)(128)(4,1)} %bitcast.76), calls=%async_computation.8 | async-start | bytes 8388608
  59.4 18.9 %slice-start.1 = ((s8[16777216]{0:T(1024)(128)(4,1)}), s8[4194304]{0:T(1024)(128)(4,1)S(1)}, s32[]{:S(2)}) async-start(s8[16777216]{0:T(1024)(128)(4,1)} %bitcast.76), calls=%async_computation.9 | async-start | bytes 8388608
  68.3 10.0 %slice-start.2 = ((s8[16777216]{0:T(1024)(128)(4,1)}), s8[4194304]{0:T(1024)(128)(4,1)S(1)}, s32[]{:S(2)}) async-start(s8[16777216]{0:T(1024)(128)(4,1)} %bitcast.76), calls=%async_computation.10 | async-start | bytes 8388608
  68.4 10.0 %slice-start.3 = ((s8[16777216]{0:T(1024)(128)(4,1)}), s8[4194304]{0:T(1024)(128)(4,1)S(1)}, s32[]{:S(2)}) async-start(s8[16777216]{0:T(1024)(128)(4,1)} %bitcast.76), calls=%async_computation.11 | async-start | bytes 8388608
  82.4 27.0 %all-to-all-start.1 = ((f32[8,8,4096]{2,1,0:T(8,128)}), f32[8,8,4096]{2,1,0:T(8,128)S(1)}, u32[]{:S(2)}, u32[]{:S(2)}) async-start(f32[8,8,4096]{2,1,0:T(8,128)} %fusion), calls=%async_computation.1 | async-start | bytes 2097152 | tf_op jit(solution)/shard_map/all_to_all | solution.py:126
  86.3 27.3 %copy-start.1 = (s32[28,2]{0,1:T(2,128)S(1)}, s32[28,2]{0,1:T(2,128)}, u32[]{:S(2)}) copy-start(s32[28,2]{0,1:T(2,128)} %param.9) | copy-start | bytes 676
  109.4 19.6 %all-to-all-start.3 = ((f32[8,8,4096]{2,1,0:T(8,128)}), f32[8,8,4096]{2,1,0:T(8,128)S(1)}, u32[]{:S(2)}, u32[]{:S(2)}) async-start(f32[8,8,4096]{2,1,0:T(8,128)} %fusion.15), calls=%async_computation.4 | async-start | bytes 2097152 | tf_op jit(solution)/shard_map/all_to_all | solution.py:133
  113.6 33.8 %reduce-scatter.3.cloned.1.call-start = ((), (), s32[]{:S(2)}) async-start(), calls=%async_computation.6 | async-start | bytes 327680 | tf_op jit(solution)/shard_map/reduce_scatter | solution.py:144
  115.3 15.1 %copy-start = (bf16[64,2048]{1,0:T(8,128)(2,1)S(1)}, bf16[64,2048]{1,0:T(8,128)(2,1)}, u32[]{:S(2)}) copy-start(bf16[64,2048]{1,0:T(8,128)(2,1)} %get-tuple-element.9) | copy-start | bytes 786436
  115.3 43.7 %reduce-scatter.5.cloned.1.call-start = ((), (), s32[]{:S(2)}) async-start(), calls=%async_computation.7 | async-start | bytes 327680 | tf_op jit(solution)/shard_map/reduce_scatter | solution.py:147
Sparse Core Ops, SparseCore 0:
  117.2 20.6 reduce-scatter.2
  140.7 18.2 reduce-scatter.4
